TPU v7x, 32 devices: a whole 2x2x4 slice. The times are simulated.
32 devices in a mesh: gx: 8 (over y, x, core), yz: 4 (over z).
Axes of the slice: x: 2, y: 2, z: 4, core: 2. Of those that a mesh axis runs over, the one named last changes fastest.
Arguments:
- vel: float32 [3, 48, 192, 1024], P(None, 'gx', 'yz'), may hold values from -6 to 6
- q_old: float32 [3, 48, 192, 1024], P(None, 'gx', None, 'yz'), may hold values from -6 to 6
- pressure_guess: float32 [48, 192, 1024], P('gx', None, 'yz'), may hold values from -6 to 6
- shear_shift: int32 [1], replicated, may hold values from 0 to 1023
Outputs:
- vel_next: float32 [3, 48, 192, 1024], P(None, 'gx', 'yz')
- q_next: float32 [3, 48, 192, 1024], P(None, 'gx', None, 'yz')
- pressure: float32 [48, 192, 1024], P('gx', None, 'yz')
All inputs are finite; a program needn't handle non-finite values.
Results may differ from a plain program's by a relative error of at most 0.00013.
Values sent between devices are 32-bit elements; how exact they have to be, the bound alone decides.
No kernel may reach another device: no remote copies, remote signals or barrier semaphores. Data moves between devices by JAX's collectives and lax.ppermute only.
A program may use at most 128 MiB of HBM per device.

v0:
```python
import math
import jax
import jax.numpy as jnp
from jax import lax
from jax.sharding import PartitionSpec as P

SWEEPS = 2
highest = lax.Precision.HIGHEST
viscosity = 0.05
time_step = 0.2
keep_weight = -5.0 / 9.0
section_weight = 15.0 / 16.0
shear_param = 1.5
fraction = 0.375


def padded_2(cells, sides, width):
    for axis, dim in sides:
        count = lax.axis_size(axis)
        head = lax.slice_in_dim(cells, 0, width, axis=dim)
        tail = lax.slice_in_dim(cells, cells.shape[dim] - width, cells.shape[dim], axis=dim)
        cells = jnp.concatenate(
            [
                lax.ppermute(tail, axis, [(i, (i + 1) % count) for i in range(count)]),
                cells,
                lax.ppermute(head, axis, [((i + 1) % count, i) for i in range(count)]),
            ],
            axis=dim,
        )
    return cells


def split_parts(packed, block_len):
    shaped = packed.reshape(packed.shape[:-1] + (packed.shape[-1] // (2 * block_len), 2, block_len))
    return (shaped[..., 0:1, :], shaped[..., 1:2, :])


def join_parts(real_part, imag_part, shape):
    return jnp.concatenate([real_part, imag_part], axis=-2).reshape(shape)


def turn(packed, wave, block_len):
    real_part, imag_part = split_parts(packed, block_len)
    return join_parts(-wave * imag_part, wave * real_part, packed.shape)


def scale_modes(packed, factor, block_len):
    real_part, imag_part = split_parts(packed, block_len)
    return join_parts(factor * real_part, factor * imag_part, packed.shape)


def rotate(packed, cosine, sine, block_len):
    real_part, imag_part = split_parts(packed, block_len)
    return join_parts(
        real_part * cosine - imag_part * sine, real_part * sine + imag_part * cosine, packed.shape
    )


def z_apply(packed, cos_z, sin_z, block_len, sign):
    with_cos = jnp.einsum("wz,nxzk->nxwk", cos_z, packed, precision=highest)
    with_sin = jnp.einsum("wz,nxzk->nxwk", sin_z, packed, precision=highest)
    real_part = with_cos[..., :block_len] + sign * with_sin[..., block_len:]
    imag_part = with_cos[..., block_len:] - sign * with_sin[..., :block_len]
    return jnp.concatenate([real_part, imag_part], axis=-1)


def x_slice(padded, offset, rows_x):
    return padded[:, 3 + offset : 3 + offset + rows_x]


def first_diff(padded, rows_x):
    return (
        45.0 * (x_slice(padded, 1, rows_x) - x_slice(padded, -1, rows_x))
        - 9.0 * (x_slice(padded, 2, rows_x) - x_slice(padded, -2, rows_x))
        + (x_slice(padded, 3, rows_x) - x_slice(padded, -3, rows_x))
    ) / 60.0


def second_diff(padded, rows_x):
    return (
        2.0 * (x_slice(padded, 3, rows_x) + x_slice(padded, -3, rows_x))
        - 27.0 * (x_slice(padded, 2, rows_x) + x_slice(padded, -2, rows_x))
        + 270.0 * (x_slice(padded, 1, rows_x) + x_slice(padded, -1, rows_x))
        - 490.0 * x_slice(padded, 0, rows_x)
    ) / 180.0


def local(vel, q_old, pressure_guess, shear_shift):
    rows_x = vel.shape[1]
    width_y = vel.shape[3]
    depth_z = q_old.shape[2]
    groups = lax.axis_size("yz")
    block_len = width_y // (2 * groups)
    group_id = lax.axis_index("yz")
    slab_id = lax.axis_index("gx")
    slabs = lax.axis_size("gx")
    total_x = rows_x * slabs
    offset = shear_shift[0]
    padded = padded_2(vel, (("gx", 1),), 3)
    tail_rows = padded[:, :3]
    front_rows = padded[:, rows_x + 3 :]
    moved_tail = (1.0 - fraction) * jnp.roll(tail_rows, -offset, axis=3) + fraction * jnp.roll(
        tail_rows, -offset - 1, axis=3
    )
    moved_front = (1.0 - fraction) * jnp.roll(front_rows, offset, axis=3) + fraction * jnp.roll(
        front_rows, offset + 1, axis=3
    )
    tail_rows = jnp.where(slab_id == 0, moved_tail, tail_rows)
    front_rows = jnp.where(slab_id == slabs - 1, moved_front, front_rows)
    padded = jnp.concatenate([tail_rows, vel, front_rows], axis=1)
    omega = 2.0 / total_x
    xpos = (
        (slab_id * rows_x + jnp.arange(rows_x, dtype=jnp.int32)).astype(jnp.float32)
        + 0.5
        - total_x / 2.0
    )
    background = (-shear_param * omega * xpos)[:, None, None]
    coriolis = jnp.stack(
        [2.0 * omega * vel[1], -(2.0 - shear_param) * omega * vel[0], jnp.zeros_like(vel[0])]
    )
    term_a = (
        -first_diff(padded * padded[0][None], rows_x)
        + viscosity * second_diff(padded, rows_x)
        + coriolis
    )
    term_b = -(vel[1] + background)[None] * vel
    term_c = -vel[2][None] * vel
    columns = jnp.arange(width_y, dtype=jnp.int32)
    part_id = columns // block_len % 2
    mode_col = columns // (2 * block_len) * block_len + columns % block_len
    angle_y = (
        2.0
        * math.pi
        / width_y
        * (columns[:, None] * mode_col[None, :] % width_y).astype(jnp.float32)
    )
    forward_y = jnp.where(part_id[None, :] == 0, jnp.cos(angle_y), -jnp.sin(angle_y)) / math.sqrt(
        width_y
    )

    def to_modes(field):
        flat = field.reshape(-1, width_y)
        return jnp.dot(
            flat, forward_y, precision=highest, preferred_element_type=jnp.float32
        ).reshape(field.shape)

    spec_a = to_modes(term_a)
    spec_b = to_modes(term_b)
    spec_c = to_modes(term_c)
    spec_u = to_modes(vel)
    cells_z = jnp.arange(depth_z, dtype=jnp.int32)
    angle_z = (
        2.0
        * math.pi
        / depth_z
        * (cells_z[:, None] * cells_z[None, :] % depth_z).astype(jnp.float32)
    )
    cos_z = jnp.cos(angle_z) / math.sqrt(depth_z)
    sin_z = jnp.sin(angle_z) / math.sqrt(depth_z)
    signed_z = jnp.where(cells_z < depth_z // 2, cells_z, cells_z - depth_z)
    wave_z = (2.0 * math.pi / depth_z * signed_z.astype(jnp.float32)).reshape(depth_z, 1, 1, 1)
    own_modes = group_id * block_len + jnp.arange(block_len, dtype=jnp.int32)
    own_wave = (2.0 * math.pi / width_y * own_modes.astype(jnp.float32)).reshape(1, 1, block_len)
    all_wave = (
        2.0
        * math.pi
        / width_y
        * jnp.arange(groups * block_len, dtype=jnp.int32).astype(jnp.float32)
    ).reshape(groups, 1, block_len)
    combined = (
        spec_a
        + turn(spec_b, all_wave, block_len)
        - viscosity * scale_modes(spec_u, all_wave * all_wave, block_len)
    )
    spectral = z_apply(
        lax.all_to_all(combined, "yz", split_axis=3, concat_axis=2, tiled=True),
        cos_z,
        sin_z,
        block_len,
        1.0,
    )
    spectral = spectral + turn(
        z_apply(
            lax.all_to_all(spec_c, "yz", split_axis=3, concat_axis=2, tiled=True),
            cos_z,
            sin_z,
            block_len,
            1.0,
        ),
        wave_z,
        block_len,
    )
    tendency = spectral - viscosity * scale_modes(
        z_apply(
            lax.all_to_all(spec_u, "yz", split_axis=3, concat_axis=2, tiled=True),
            cos_z,
            sin_z,
            block_len,
            1.0,
        ),
        wave_z * wave_z,
        block_len,
    )
    edge_angle = (
        2.0
        * math.pi
        / width_y
        * (
            (own_modes * offset % width_y).astype(jnp.float32)
            + fraction * own_modes.astype(jnp.float32)
        )
    )
    edge_cos = jnp.cos(edge_angle).reshape(1, 1, block_len)
    edge_sin = jnp.sin(edge_angle).reshape(1, 1, block_len)

    def fix_edges(stacked, depth_x):
        extent = stacked.shape[1]
        lower = stacked[:, :depth_x]
        upper = stacked[:, extent - depth_x :]
        middle = stacked[:, depth_x : extent - depth_x]
        lower = jnp.where(slab_id == 0, rotate(lower, edge_cos, edge_sin, block_len), lower)
        upper = jnp.where(
            slab_id == slabs - 1, rotate(upper, edge_cos, -edge_sin, block_len), upper
        )
        return jnp.concatenate([lower, middle, upper], axis=1)

    denom_half = (
        2.0
        + own_wave.reshape(1, block_len) * own_wave.reshape(1, block_len)
        + wave_z.reshape(depth_z, 1) * wave_z.reshape(depth_z, 1)
    )
    denom = jnp.concatenate([denom_half, denom_half], axis=-1)

    def faces(stacked):
        return fix_edges(padded_2(stacked, (("gx", 1),), 1), 1)

    first = faces(jnp.stack([tendency[0], pressure_guess]))
    along_x = first[0]
    press = first[1]
    diverge = (
        0.5 * (along_x[2:] - along_x[:-2])
        + turn(tendency[1], own_wave, block_len)
        + turn(tendency[2], wave_z, block_len)
    )
    for sweep_no in range(SWEEPS):
        if sweep_no > 0:
            press = faces(press[None])[0]
        press = (press[2:] + press[:-2] - diverge) / denom
    ghosted_p = faces(press[None])[0]
    slope_x = 0.5 * (ghosted_p[2:] - ghosted_p[:-2])
    gradient = jnp.stack(
        [slope_x, turn(press, own_wave, block_len), turn(press, wave_z, block_len)]
    )
    q_next = keep_weight * q_old + time_step * (tendency - gradient)
    spatial = z_apply(q_next, cos_z, sin_z, block_len, -1.0)
    weights = jnp.where(mode_col == 0, 1.0, 2.0).astype(jnp.float32)
    inverse_y = (
        jnp.where(part_id[:, None] == 0, jnp.cos(angle_y.T), -jnp.sin(angle_y.T))
        * weights[:, None]
        / math.sqrt(width_y)
    )
    piece = lax.all_to_all(spatial, "yz", split_axis=2, concat_axis=3, tiled=True)
    flat = piece.reshape(-1, width_y)
    correction = jnp.dot(
        flat, inverse_y, precision=highest, preferred_element_type=jnp.float32
    ).reshape(piece.shape)
    vel_next = vel + section_weight * correction
    return (vel_next, q_next, press)


def solution(mesh):
    placed = (P(None, "gx", "yz", None), P(None, "gx", None, "yz"), P("gx", None, "yz"), P())
    return jax.shard_map(
        local,
        mesh=mesh,
        in_specs=placed,
        out_specs=(P(None, "gx", "yz", None), P(None, "gx", None, "yz"), P("gx", None, "yz")),
        check_vma=False,
    )
```

profile of v0, /device:TPU:3, one launch (start us, length us, event | category | flops | bytes accessed | tf_op | source)
XLA Modules:
  0.0 829.1 jit_solution(1366526000127523778)
XLA Ops:
  0.7 4.5 slice_multiply_fusion.11
  6.0 29.1 %fusion.13 = f32[3,6,48,1024]{3,2,1,0:T(8,128)} fusion(s32[1024]{0:T(1024)S(1)} %fusion.193, pred[1024]{0:T(1024)(128)(4,1)S(1)} %fusion.190, f32[3,6,48,1024]{3,2,1,0:T(8,128)S(1)} %fusion.327), kind=kOutput, calls=%fused_computation.31 | convolution fusion | flops 10889461760 | bytes 7083008 | tf_op jit(solution)/shard_map/dot_general | solution.py:143
  35.1 8.8 %copy.33 = f32[3,6,48,1024]{2,1,0,3:T(8,128)} copy(f32[3,6,48,1024]{3,2,1,0:T(8,128)} %fusion.13) | data formatting | bytes 7077888 | tf_op jit(solution)/shard_map/dot_general | solution.py:143
  43.9 11.7 %reshape.517 = f32[4,1,221184]{2,1,0:T(1,128)} reshape(f32[1024,3,6,48]{3,2,1,0:T(8,128)} %bitcast.207) | data formatting | bytes 7077888
  55.6 4.7 all-to-all-start.1
  65.6 16.9 %select_multiply_fusion.6 = f32[1024,1024]{1,0:T(8,128)S(1)} fusion(s32[1024]{0:T(1024)S(1)} %fusion.193, pred[1024]{0:T(1024)(128)(4,1)S(1)} %fusion.190), kind=kLoop, calls=%fused_computation.50.clone.1.clone.1 | loop fusion | flops 17825792 | bytes 4199424 | tf_op jit(solution)/shard_map/dot_general | solution.py:143
  82.5 13.4 %fusion.104 = f32[1024,864]{0,1:T(8,128)} fusion(f32[864,1024]{1,0:T(8,128)S(1)} %bitcast.206, f32[1024,1024]{1,0:T(8,128)S(1)} %select_multiply_fusion.6), kind=kOutput, calls=%fused_computation.128 | convolution fusion | flops 10871635968 | bytes 11272192 | tf_op jit(solution)/shard_map/dot_general | solution.py:143
  96.0 5.8 reshape_reshape.2
  101.7 8.8 %copy.35 = f32[3,6,48,1024]{2,1,0,3:T(8,128)} copy(f32[3,6,48,1024]{3,2,1,0:T(8,128)} %bitcast.221) | data formatting | bytes 7077888 | tf_op jit(solution)/shard_map/reshape | solution.py:145
  110.5 11.7 %reshape.515 = f32[4,1,221184]{2,1,0:T(1,128)} reshape(f32[1024,3,6,48]{3,2,1,0:T(8,128)} %bitcast.208) | data formatting | bytes 7077888
  124.6 40.5 %fusion.11 = f32[3,6,48,4,2,128]{5,2,4,3,1,0:T(8,128)S(1)} fusion(s32[4,2,128]{2,1,0:T(2,128)S(1)} %fusion.195, pred[4,2,128]{2,1,0:T(4,128)(4,1)S(1)} %fusion.199, f32[3,6,48,1024,1,1]{3,2,5,4,1,0:T(8,128)S(1)} %fusion.325), kind=kOutput, calls=%fused_computation.29 | convolution fusion | flops 10889461760 | bytes 7083008 | tf_op jit(solution)/shard_map/dot_general | solution.py:143
  172.6 5.4 maximum_multiply_fusion
  178.0 5.0 all-to-all-start.2
  183.6 5.7 copy.30
  189.3 5.7 reshape.486
  194.9 5.6 mul.836
  216.0 8.3 fusion.331
  224.3 31.9 %add_subtract_fusion = f32[3,6,48,1024]{3,2,1,0:T(8,128)} fusion(f32[3,6,48,1024]{3,2,1,0:T(8,128)} %mul.836, f32[3,6,48,1024]{3,2,1,0:T(8,128)} %reshape.486, s32[1024]{0:T(1024)S(1)} %fusion.193, pred[1024]{0:T(1024)(128)(4,1)S(1)} %copy-done.33, f32[3,6,48,1024]{3,2,1,0:T(8,128)} %fusion.331), kind=kOutput, calls=%fused_computation.108 | convolution fusion | flops 10891231232 | bytes 14160896 | tf_op jit(solution)/shard_map/dot_general | solution.py:143
  256.3 8.8 %copy.31 = f32[3,6,48,1024]{2,1,0,3:T(8,128)} copy(f32[3,6,48,1024]{3,2,1,0:T(8,128)} %add_subtract_fusion) | data formatting | bytes 7077888 | tf_op jit(solution)/shard_map/sub | solution.py:171
  265.0 11.7 %reshape.519 = f32[4,1,221184]{2,1,0:T(1,128)} reshape(f32[1024,3,6,48]{3,2,1,0:T(8,128)} %bitcast.209) | data formatting | bytes 7077888
  276.7 5.2 all-to-all-start
  283.0 40.4 %reduce.1 = f32[4,221184]{1,0:T(4,128)} reduce(f32[4,1,221184]{2,1,0:T(1,128)} %all-to-all-done.1, f32[]{:T(128)} %broadcast.808), dimensions={1}, to_apply=%all_to_all.54.reduce_sub_computation | reduce | bytes 7077892 | tf_op jit(solution)/shard_map/all_to_all | solution.py:184
  323.4 14.8 %reshape.518 = f32[1024,3,6,48]{3,2,1,0:T(8,128)} reshape(f32[4,221184]{1,0:T(4,128)} %reduce.1) | data formatting | bytes 7077888
  338.2 8.7 %copy.34 = f32[3,6,48,4,256]{4,2,3,1,0:T(8,128)} copy(f32[3,6,48,4,256]{2,1,0,4,3:T(8,128)} %bitcast.210) | data formatting | bytes 7077888 | tf_op jit(solution)/shard_map/all_to_all | solution.py:184
  347.0 6.5 convolution_bitcast_fusion.4
  360.4 5.3 reshape.488
  365.8 6.6 slice_multiply_fusion.5
  372.3 5.0 pad_maximum_fusion.6
  377.4 5.6 reshape.489
  383.0 40.8 %reduce = f32[4,221184]{1,0:T(4,128)} reduce(f32[4,1,221184]{2,1,0:T(1,128)} %all-to-all-done.2, f32[]{:T(128)} %broadcast.808), dimensions={1}, to_apply=%all_to_all.58.reduce_sub_computation | reduce | bytes 7077892 | tf_op jit(solution)/shard_map/all_to_all | solution.py:195
  423.9 14.8 %reshape.516 = f32[1024,3,6,48]{3,2,1,0:T(8,128)} reshape(f32[4,221184]{1,0:T(4,128)} %reduce) | data formatting | bytes 7077888
  438.6 8.7 %copy.36 = f32[3,6,48,4,256]{4,2,3,1,0:T(8,128)} copy(f32[3,6,48,4,256]{2,1,0,4,3:T(8,128)} %bitcast.211) | data formatting | bytes 7077888 | tf_op jit(solution)/shard_map/all_to_all | solution.py:195
  447.4 6.5 convolution_bitcast_fusion.2
  460.8 5.3 reshape.491
  466.2 6.6 slice_multiply_fusion.3
  472.7 5.5 maximum_multiply_fusion.1
  478.2 5.6 mul.857
  483.8 40.8 %reduce.2 = f32[4,221184]{1,0:T(4,128)} reduce(f32[4,1,221184]{2,1,0:T(1,128)} %all-to-all-done, f32[]{:T(128)} %broadcast.808), dimensions={1}, to_apply=%all_to_all.50.reduce_sub_computation | reduce | bytes 7077892 | tf_op jit(solution)/shard_map/all_to_all | solution.py:176
  524.7 14.8 %reshape.520 = f32[1024,3,6,48]{3,2,1,0:T(8,128)} reshape(f32[4,221184]{1,0:T(4,128)} %reduce.2) | data formatting | bytes 7077888
  539.5 8.7 %copy.32 = f32[3,6,48,4,256]{4,2,3,1,0:T(8,128)} copy(f32[3,6,48,4,256]{2,1,0,4,3:T(8,128)} %bitcast.212) | data formatting | bytes 7077888 | tf_op jit(solution)/shard_map/all_to_all | solution.py:176
  548.2 6.5 convolution_bitcast_fusion.6
  689.0 4.5 copy.61
  693.6 5.1 all-to-all-start.3
  698.7 19.5 %fusion.329 = f32[1024,1024,1,1]{1,0,3,2:T(8,128)} fusion(f32[1024]{0:T(1024)S(1)} %compare_select_fusion.2, s32[1024]{0:T(1024)S(1)} %fusion.193, pred[1024]{0:T(1024)(128)(4,1)S(1)} %copy-done.34), kind=kLoop, calls=%fused_computation.28.clone.clone.clone.1 | loop fusion | flops 18874368 | bytes 4203520 | tf_op jit(solution)/shard_map/dot_general | solution.py:264
  718.2 83.7 %all-to-all-done.3 = f32[3,6,192,256]{3,1,0,2:T(8,128)} async-done(((f32[3,6,192,256]{3,1,0,2:T(8,128)}), f32[3,6,192,256]{3,1,0,2:T(8,128)}, u32[]{:S(2)}, u32[]{:S(2)}) %all-to-all-start.3) | async-done | bytes 3538976 | tf_op jit(solution)/shard_map/all_to_all | solution.py:262
  801.9 6.4 copy.88
  808.3 5.3 dot_general.56
  813.6 15.2 %multiply_add_fusion = f32[3,6,48,1024]{3,2,1,0:T(8,128)} fusion(f32[3,6,48,1024]{3,2,1,0:T(8,128)S(1)} %copy-done, f32[3,6,48,1024]{3,2,1,0:T(8,128)} %dot_general.56, f32[1024,1024,1,1]{1,0,3,2:T(8,128)} %fusion.329), kind=kOutput, calls=%fused_computation.106 | convolution fusion | flops 10873405440 | bytes 14811136 | tf_op jit(solution)/shard_map/dot_general | solution.py:264
  (202 shorter events, 180.0 us)
Async XLA Ops:
  0.7 65.0 %copy-start.32 = (pred[1024]{0:T(1024)(128)(4,1)}, pred[1024]{0:T(1024)(128)(4,1)S(1)}, u32[]{:S(2)}) copy-start(pred[1024]{0:T(1024)(128)(4,1)S(1)} %fusion.190) | copy-start | bytes 3076
  0.7 4.5 copy-start
  55.6 122.4 %all-to-all-start.1 = ((f32[4,1,221184]{2,1,0:T(1,128)}), f32[4,1,221184]{2,1,0:T(1,128)}, u32[]{:S(2)}, u32[]{:S(2)}) async-start(f32[4,1,221184]{2,1,0:T(1,128)} %reshape.517), calls=%async_computation.1 | async-start | bytes 7077888 | tf_op jit(solution)/shard_map/all_to_all | solution.py:184
  62.6 139.4 %collective-permute-start = (f32[3,3,48,1024]{3,2,1,0:T(8,128)}, f32[3,3,48,1024]{3,2,1,0:T(8,128)}, u32[]{:S(2)}, u32[]{:S(2)}) collective-permute-start(f32[3,3,48,1024]{3,2,1,0:T(8,128)} %get-tuple-element.30), channel_id=1, source_target_pairs={{0,4},{4,8},{8,12},{12,16},{16,20},{20,24},{24,28},{28,0},{1,5},{5... | collective-permute-start | bytes 5308424 | tf_op jit(solution)/shard_map/ppermute | solution.py:24
  64.5 140.9 %collective-permute-start.1 = (f32[3,3,48,1024]{3,2,1,0:T(8,128)}, f32[3,3,48,1024]{3,2,1,0:T(8,128)}, u32[]{:S(2)}, u32[]{:S(2)}) collective-permute-start(f32[3,3,48,1024]{3,2,1,0:T(8,128)} %get-tuple-element.29), channel_id=1, source_target_pairs={{4,0},{8,4},{12,8},{16,12},{20,16},{24,20},{28,24},{0,28},{5,1},{9... | collective-permute-start | bytes 5308424 | tf_op jit(solution)/shard_map/ppermute | solution.py:26
  165.6 3.3 copy-start.10
  178.0 98.7 %all-to-all-start.2 = ((f32[4,1,221184]{2,1,0:T(1,128)}), f32[4,1,221184]{2,1,0:T(1,128)}, u32[]{:S(2)}, u32[]{:S(2)}) async-start(f32[4,1,221184]{2,1,0:T(1,128)} %reshape.515), calls=%async_computation.2 | async-start | bytes 7077888 | tf_op jit(solution)/shard_map/all_to_all | solution.py:195
  216.0 8.3 %copy-start.33 = (pred[1024]{0:T(1024)(128)(4,1)S(1)}, pred[1024]{0:T(1024)(128)(4,1)}, u32[]{:S(2)}) copy-start(pred[1024]{0:T(1024)(128)(4,1)} %copy-done.32) | copy-start | bytes 3076
  276.7 207.1 %all-to-all-start = ((f32[4,1,221184]{2,1,0:T(1,128)}), f32[4,1,221184]{2,1,0:T(1,128)}, u32[]{:S(2)}, u32[]{:S(2)}) async-start(f32[4,1,221184]{2,1,0:T(1,128)} %reshape.519), calls=%async_computation | async-start | bytes 7077888 | tf_op jit(solution)/shard_map/all_to_all | solution.py:176
  347.0 6.5 copy-start.4
  447.4 6.5 copy-start.5
  548.2 6.5 copy-start.6
  559.1 2.0 copy-start.8
  559.1 3.1 copy-start.9
  562.9 2.5 copy-start.1
  562.9 3.6 copy-start.24
  565.4 1.0 copy-start.11
  567.4 28.1 %collective-permute-start.2 = (f32[2,1,192,256]{3,2,1,0:T(8,128)}, f32[2,1,192,256]{3,2,1,0:T(8,128)}, u32[]{:S(2)}, u32[]{:S(2)}) collective-permute-start(f32[2,1,192,256]{3,2,1,0:T(8,128)} %get-tuple-element.35), channel_id=1, source_target_pairs={{4,0},{8,4},{12,8},{16,12},{20,16},{24,20},{28,24},{0,28},{5,1},{9... | collective-permute-start | bytes 1179656 | tf_op jit(solution)/shard_map/ppermute | solution.py:26
  568.7 31.0 %collective-permute-start.3 = (f32[2,1,192,256]{3,2,1,0:T(8,128)}, f32[2,1,192,256]{3,2,1,0:T(8,128)}, u32[]{:S(2)}, u32[]{:S(2)}) collective-permute-start(f32[2,1,192,256]{3,2,1,0:T(8,128)} %get-tuple-element.36), channel_id=1, source_target_pairs={{0,4},{4,8},{8,12},{12,16},{16,20},{20,24},{24,28},{28,0},{1,5},{5... | collective-permute-start | bytes 1179656 | tf_op jit(solution)/shard_map/ppermute | solution.py:24
  603.1 4.1 copy-start.12
  603.1 4.1 copy-start.13
  603.2 4.1 copy-start.15
  603.2 4.1 copy-start.25
  603.2 4.1 copy-start.27
  607.3 3.3 copy-start.35
  608.8 1.0 copy-start.18
  610.6 13.1 %collective-permute-start.4 = (f32[1,1,192,256]{3,2,1,0:T(8,128)}, f32[1,1,192,256]{3,2,1,0:T(8,128)}, u32[]{:S(2)}, u32[]{:S(2)}) collective-permute-start(f32[1,1,192,256]{3,2,1,0:T(8,128)} %get-tuple-element.43), channel_id=1, source_target_pairs={{4,0},{8,4},{12,8},{16,12},{20,16},{24,20},{28,24},{0,28},{5,1},{9... | collective-permute-start | bytes 589832 | tf_op jit(solution)/shard_map/ppermute | solution.py:26
  615.2 15.1 %copy-start.29 = (f32[128]{0:T(128)S(1)}, f32[128]{0:T(128)}, u32[]{:S(2)}) copy-start(f32[128]{0:T(128)} %get-tuple-element.8) | copy-start | bytes 1540
  618.3 9.0 %collective-permute-start.5 = (f32[1,1,192,256]{3,2,1,0:T(8,128)}, f32[1,1,192,256]{3,2,1,0:T(8,128)}, u32[]{:S(2)}, u32[]{:S(2)}) collective-permute-start(f32[1,1,192,256]{3,2,1,0:T(8,128)} %get-tuple-element.44), channel_id=1, source_target_pairs={{0,4},{4,8},{8,12},{12,16},{16,20},{20,24},{24,28},{28,0},{1,5},{5... | collective-permute-start | bytes 589832 | tf_op jit(solution)/shard_map/ppermute | solution.py:24
  629.0 4.7 copy-start.7
  629.0 4.7 copy-start.19
  629.0 4.7 copy-start.26
  629.0 4.7 copy-start.28
  633.7 3.8 copy-start.14
  633.7 3.8 copy-start.16
  636.5 1.0 copy-start.17
  641.6 8.6 %copy-start.36 = (f32[128]{0:T(128)S(1)}, f32[128]{0:T(128)}, u32[]{:S(2)}) copy-start(f32[128]{0:T(128)} %get-tuple-element.85) | copy-start | bytes 1540
  641.6 8.6 %copy-start.37 = (f32[128]{0:T(128)S(1)}, f32[128]{0:T(128)}, u32[]{:S(2)}) copy-start(f32[128]{0:T(128)} %fusion.278) | copy-start | bytes 1540
  643.4 21.0 %collective-permute-start.6 = (f32[1,1,192,256]{3,2,1,0:T(8,128)}, f32[1,1,192,256]{3,2,1,0:T(8,128)}, u32[]{:S(2)}, u32[]{:S(2)}) collective-permute-start(f32[1,1,192,256]{3,2,1,0:T(8,128)} %get-tuple-element.37), channel_id=1, source_target_pairs={{4,0},{8,4},{12,8},{16,12},{20,16},{24,20},{28,24},{0,28},{5,1},{9... | collective-permute-start | bytes 589832 | tf_op jit(solution)/shard_map/ppermute | solution.py:26
  643.4 24.6 %collective-permute-start.7 = (f32[1,1,192,256]{3,2,1,0:T(8,128)}, f32[1,1,192,256]{3,2,1,0:T(8,128)}, u32[]{:S(2)}, u32[]{:S(2)}) collective-permute-start(f32[1,1,192,256]{3,2,1,0:T(8,128)} %get-tuple-element.38), channel_id=1, source_target_pairs={{0,4},{4,8},{8,12},{12,16},{16,20},{20,24},{24,28},{28,0},{1,5},{5... | collective-permute-start | bytes 589832 | tf_op jit(solution)/shard_map/ppermute | solution.py:24
  657.9 13.2 %copy-start.30 = (f32[128]{0:T(128)S(1)}, f32[128]{0:T(128)}, u32[]{:S(2)}) copy-start(f32[128]{0:T(128)} %get-tuple-element.9) | copy-start | bytes 1540
  657.9 13.2 %copy-start.31 = (f32[128]{0:T(128)S(1)}, f32[128]{0:T(128)}, u32[]{:S(2)}) copy-start(f32[128]{0:T(128)} %get-tuple-element.83) | copy-start | bytes 1540
  669.7 6.9 copy-start.2
  669.7 6.9 copy-start.22
  669.7 6.9 copy-start.23
  679.5 4.4 copy-start.3
  693.6 5.1 copy-start.34
  693.6 108.3 %all-to-all-start.3 = ((f32[3,6,192,256]{3,1,0,2:T(8,128)}), f32[3,6,192,256]{3,1,0,2:T(8,128)}, u32[]{:S(2)}, u32[]{:S(2)}) async-start(f32[3,6,192,256]{3,1,0,2:T(8,128)} %copy.61), calls=%async_computation.3 | async-start | bytes 9437184 | tf_op jit(solution)/shard_map/all_to_all | solution.py:262
  (2 other events, 1.8 us)
where the time goes:
time: 841 us; the launch traced here: 829 us
  other arithmetic  272 us (32%)
  local copies, waits for them, and re-layouts  268 us (32%)
  matrix products  172 us (20%)
  waiting for transfers between devices  83.7 us (10%)
  starting transfers between devices  30.9 us (4%)
    dot_general x4, matrix products, to_modes(): jnp.dot(flat, forward_y, precision=highest, preferred_element_type=jnp.fl...  115 us
    unnamed x84, local copies, waits for them, and re-layouts  91.6 us
    all_to_all x1, waiting for transfers between devices, local(): lax.all_to_all(spatial, 'yz', split_axis=2, concat_axis=3, tiled=True)  83.7 us
    all_to_all x1, other arithmetic, local(): lax.all_to_all(combined, 'yz', split_axis=3, concat_axis=2, tiled=True)  40.8 us
    all_to_all x1, other arithmetic, local(): lax.all_to_all(spec_u, 'yz', split_axis=3, concat_axis=2, tiled=True)  40.8 us
    all_to_all x1, other arithmetic, local(): lax.all_to_all(spec_c, 'yz', split_axis=3, concat_axis=2, tiled=True)  40.4 us
    dot_general x4, other arithmetic, to_modes(): jnp.dot(flat, forward_y, precision=highest, preferred_element_type=jnp.fl...  27.8 us
    reshape x6, local copies, waits for them, and re-layouts, join_parts(): return jnp.concatenate([real_part, imag_part], axis=-2).reshape(shape)  24.1 us
  transfers between devices with their start and end apart: 12, of which 1 were waited for; matrix products, arithmetic and copies ran while one was open for 59% of the time, Pallas kernels for 0%

commit v1 on v0

--- a/solution.py
+++ b/solution.py
@@ -3,6 +3,7 @@
 import jax.numpy as jnp
 from jax import lax
 from jax.sharding import PartitionSpec as P
+from jax.lax import all_to_all, axis_size
 
 SWEEPS = 2
 highest = lax.Precision.HIGHEST
@@ -259,7 +260,9 @@
         * weights[:, None]
         / math.sqrt(width_y)
     )
-    piece = lax.all_to_all(spatial, "yz", split_axis=2, concat_axis=3, tiled=True)
+    part_next = axis_size("yz")
+    before = jnp.stack(jnp.split(spatial, part_next, 2), axis=0)
+    piece = jnp.concatenate(all_to_all(before, "yz", 0, 0), axis=3)
     flat = piece.reshape(-1, width_y)
     correction = jnp.dot(
         flat, inverse_y, precision=highest, preferred_element_type=jnp.float32

time: 841 us -> 803 us (0.955)
  waiting for transfers between devices: 83.7 us -> 58.6 us
  local copies, waits for them, and re-layouts: 268 us -> 256 us
    all_to_all x1, waiting for transfers between devices: 83.7 us -> 58.5 us  [local(): piece = jnp.concatenate(all_to_all(before, 'yz', 0, 0), axis=3)]
    unnamed x84 -> x86, local copies, waits for them, and re-layouts: 91.6 us -> 92.3 us
  transfers between devices with their start and end apart: 12 -> 12, of which waited for: 1 -> 1; matrix products, arithmetic and copies ran while one was open for 59% -> 62% of each run, Pallas kernels for 0% -> 0%
where the time goes in v1:
time: 803 us; the launch traced here: 792 us
  other arithmetic  274 us (34%)
  local copies, waits for them, and re-layouts  256 us (32%)
  matrix products  170 us (21%)
  waiting for transfers between devices  58.6 us (7%)
  starting transfers between devices  31 us (4%)
    dot_general x4, matrix products, to_modes(): jnp.dot(flat, forward_y, precision=highest, preferred_element_type=jnp.fl...  115 us
    unnamed x86, local copies, waits for them, and re-layouts  92.3 us
    all_to_all x1, waiting for transfers between devices, local(): piece = jnp.concatenate(all_to_all(before, 'yz', 0, 0), axis=3)  58.5 us
    all_to_all x1, other arithmetic, local(): lax.all_to_all(combined, 'yz', split_axis=3, concat_axis=2, tiled=True)  40.8 us
    all_to_all x1, other arithmetic, local(): lax.all_to_all(spec_u, 'yz', split_axis=3, concat_axis=2, tiled=True)  40.8 us
    all_to_all x1, other arithmetic, local(): lax.all_to_all(spec_c, 'yz', split_axis=3, concat_axis=2, tiled=True)  40.4 us
    dot_general x4, other arithmetic, to_modes(): jnp.dot(flat, forward_y, precision=highest, preferred_element_type=jnp.fl...  27.8 us
    reshape x6, local copies, waits for them, and re-layouts, join_parts(): return jnp.concatenate([real_part, imag_part], axis=-2).reshape(shape)  24.1 us
  transfers between devices with their start and end apart: 12, of which 1 were waited for; matrix products, arithmetic and copies ran while one was open for 62% of the time, Pallas kernels for 0%

profile of v1, /device:TPU:3, one launch (start us, length us, event | category | flops | bytes accessed | tf_op | source)
XLA Modules:
  0.0 791.7 jit_solution(9067445648968018792)
XLA Ops:
  0.7 4.5 slice_multiply_fusion.11
  6.0 29.1 %fusion.13 = f32[3,6,48,1024]{3,2,1,0:T(8,128)} fusion(s32[1024]{0:T(1024)S(1)} %fusion.200, pred[1024]{0:T(1024)(128)(4,1)S(1)} %fusion.197, f32[3,6,48,1024]{3,2,1,0:T(8,128)S(1)} %fusion.334), kind=kOutput, calls=%fused_computation.37 | convolution fusion | flops 10889461760 | bytes 7083008 | tf_op jit(solution)/shard_map/dot_general | solution.py:144
  35.1 9.0 %copy.35 = f32[3,6,48,1024]{2,1,0,3:T(8,128)} copy(f32[3,6,48,1024]{3,2,1,0:T(8,128)} %fusion.13) | data formatting | bytes 7077888 | tf_op jit(solution)/shard_map/dot_general | solution.py:144
  44.1 11.7 %reshape.519 = f32[4,1,221184]{2,1,0:T(1,128)} reshape(f32[1024,3,6,48]{3,2,1,0:T(8,128)} %bitcast.214) | data formatting | bytes 7077888
  55.8 4.7 all-to-all-start.1
  65.8 16.9 %select_multiply_fusion.6 = f32[1024,1024]{1,0:T(8,128)S(1)} fusion(s32[1024]{0:T(1024)S(1)} %fusion.200, pred[1024]{0:T(1024)(128)(4,1)S(1)} %fusion.197), kind=kLoop, calls=%fused_computation.56.clone.1.clone.1 | loop fusion | flops 17825792 | bytes 4199424 | tf_op jit(solution)/shard_map/dot_general | solution.py:144
  82.7 13.4 %fusion.104 = f32[1024,864]{0,1:T(8,128)} fusion(f32[864,1024]{1,0:T(8,128)S(1)} %bitcast.213, f32[1024,1024]{1,0:T(8,128)S(1)} %select_multiply_fusion.6), kind=kOutput, calls=%fused_computation.133 | convolution fusion | flops 10871635968 | bytes 11272192 | tf_op jit(solution)/shard_map/dot_general | solution.py:144
  96.1 5.8 reshape_reshape.2
  101.9 9.0 %copy.37 = f32[3,6,48,1024]{2,1,0,3:T(8,128)} copy(f32[3,6,48,1024]{3,2,1,0:T(8,128)} %bitcast.228) | data formatting | bytes 7077888 | tf_op jit(solution)/shard_map/reshape | solution.py:146
  110.9 11.7 %reshape.517 = f32[4,1,221184]{2,1,0:T(1,128)} reshape(f32[1024,3,6,48]{3,2,1,0:T(8,128)} %bitcast.215) | data formatting | bytes 7077888
  125.0 40.5 %fusion.11 = f32[3,6,48,4,2,128]{5,2,4,3,1,0:T(8,128)S(1)} fusion(s32[4,2,128]{2,1,0:T(2,128)S(1)} %fusion.202, pred[4,2,128]{2,1,0:T(4,128)(4,1)S(1)} %fusion.206, f32[3,6,48,1024,1,1]{3,2,5,4,1,0:T(8,128)S(1)} %fusion.332), kind=kOutput, calls=%fused_computation.35 | convolution fusion | flops 10889461760 | bytes 7083008 | tf_op jit(solution)/shard_map/dot_general | solution.py:144
  172.9 5.4 maximum_multiply_fusion
  178.4 5.0 all-to-all-start.2
  184.0 5.7 copy.32
  189.6 5.7 reshape.487
  195.3 5.6 mul.836
  216.4 8.3 %fusion.338 = f32[3,6,48,1024]{3,2,1,0:T(8,128)} fusion(f32[3,6,48,1024]{3,2,1,0:T(8,128)S(1)} %copy-done, f32[3,3,48,1024]{3,2,1,0:T(8,128)S(1)} %fusion.117, f32[3,3,48,1024]{3,2,1,0:T(8,128)S(1)} %fusion.115, f32[3,12,48,1024]{3,2,1,0:T(8,128)S(1)} %broadcast_multiply_fusion, f32[1,6,48,1024]{3,2,1,0:T(8,128)} %get-tuple-element.31, ...), kind=kLoop, calls=%fused_computation.70.clone.clone.clone.clone.2 | loop fusion | flops 26542080 | bytes 34209804 | tf_op jit(solution)/shard_map/dot_general | solution.py:144
  224.8 31.9 %add_subtract_fusion = f32[3,6,48,1024]{3,2,1,0:T(8,128)} fusion(f32[3,6,48,1024]{3,2,1,0:T(8,128)} %mul.836, f32[3,6,48,1024]{3,2,1,0:T(8,128)} %reshape.487, s32[1024]{0:T(1024)S(1)} %fusion.200, pred[1024]{0:T(1024)(128)(4,1)S(1)} %copy-done.34, f32[3,6,48,1024]{3,2,1,0:T(8,128)} %fusion.338), kind=kOutput, calls=%fused_computation.113 | convolution fusion | flops 10891231232 | bytes 14160896 | tf_op jit(solution)/shard_map/dot_general | solution.py:144
  256.7 9.0 %copy.33 = f32[3,6,48,1024]{2,1,0,3:T(8,128)} copy(f32[3,6,48,1024]{3,2,1,0:T(8,128)} %add_subtract_fusion) | data formatting | bytes 7077888 | tf_op jit(solution)/shard_map/sub | solution.py:172
  265.7 11.7 %reshape.521 = f32[4,1,221184]{2,1,0:T(1,128)} reshape(f32[1024,3,6,48]{3,2,1,0:T(8,128)} %bitcast.216) | data formatting | bytes 7077888
  277.3 5.2 all-to-all-start
  283.6 40.4 %reduce.1 = f32[4,221184]{1,0:T(4,128)} reduce(f32[4,1,221184]{2,1,0:T(1,128)} %all-to-all-done.1, f32[]{:T(128)} %broadcast.808), dimensions={1}, to_apply=%all_to_all.46.reduce_sub_computation | reduce | bytes 7077892 | tf_op jit(solution)/shard_map/all_to_all | solution.py:185
  324.0 14.8 %reshape.520 = f32[1024,3,6,48]{3,2,1,0:T(8,128)} reshape(f32[4,221184]{1,0:T(4,128)} %reduce.1) | data formatting | bytes 7077888
  338.8 8.7 %copy.36 = f32[3,6,48,4,256]{4,2,3,1,0:T(8,128)} copy(f32[3,6,48,4,256]{2,1,0,4,3:T(8,128)} %bitcast.217) | data formatting | bytes 7077888 | tf_op jit(solution)/shard_map/all_to_all | solution.py:185
  347.6 6.5 convolution_bitcast_fusion.4
  354.1 4.4 convolution_bitcast_fusion.5
  361.0 5.3 reshape.489
  366.3 6.6 slice_multiply_fusion.5
  372.9 5.0 pad_maximum_fusion.6
  378.0 5.6 reshape.490
  383.6 40.8 %reduce = f32[4,221184]{1,0:T(4,128)} reduce(f32[4,1,221184]{2,1,0:T(1,128)} %all-to-all-done.2, f32[]{:T(128)} %broadcast.808), dimensions={1}, to_apply=%all_to_all.50.reduce_sub_computation | reduce | bytes 7077892 | tf_op jit(solution)/shard_map/all_to_all | solution.py:196
  424.4 14.8 %reshape.518 = f32[1024,3,6,48]{3,2,1,0:T(8,128)} reshape(f32[4,221184]{1,0:T(4,128)} %reduce) | data formatting | bytes 7077888
  439.2 8.7 %copy.38 = f32[3,6,48,4,256]{4,2,3,1,0:T(8,128)} copy(f32[3,6,48,4,256]{2,1,0,4,3:T(8,128)} %bitcast.218) | data formatting | bytes 7077888 | tf_op jit(solution)/shard_map/all_to_all | solution.py:196
  448.0 6.5 convolution_bitcast_fusion.2
  454.5 4.4 convolution_bitcast_fusion.3
  461.4 5.3 reshape.492
  466.8 6.6 slice_multiply_fusion.3
  473.3 5.5 maximum_multiply_fusion.1
  478.8 5.6 mul.857
  484.4 40.8 %reduce.2 = f32[4,221184]{1,0:T(4,128)} reduce(f32[4,1,221184]{2,1,0:T(1,128)} %all-to-all-done, f32[]{:T(128)} %broadcast.808), dimensions={1}, to_apply=%all_to_all.42.reduce_sub_computation | reduce | bytes 7077892 | tf_op jit(solution)/shard_map/all_to_all | solution.py:177
  525.3 14.8 %reshape.522 = f32[1024,3,6,48]{3,2,1,0:T(8,128)} reshape(f32[4,221184]{1,0:T(4,128)} %reduce.2) | data formatting | bytes 7077888
  540.1 8.7 %copy.34 = f32[3,6,48,4,256]{4,2,3,1,0:T(8,128)} copy(f32[3,6,48,4,256]{2,1,0,4,3:T(8,128)} %bitcast.219) | data formatting | bytes 7077888 | tf_op jit(solution)/shard_map/all_to_all | solution.py:177
  548.8 6.5 convolution_bitcast_fusion.6
  680.1 4.4 convolution_bitcast_fusion
  691.7 5.2 all-to-all-start.3
  696.9 19.5 %fusion.336 = f32[1024,1024,1,1]{1,0,3,2:T(8,128)} fusion(f32[1024]{0:T(1024)S(1)} %compare_select_fusion.2, s32[1024]{0:T(1024)S(1)} %fusion.200, pred[1024]{0:T(1024)(128)(4,1)S(1)} %copy-done.35), kind=kLoop, calls=%fused_computation.34.clone.clone.clone.1 | loop fusion | flops 18874368 | bytes 4203520 | tf_op jit(solution)/shard_map/dot_general | solution.py:267
  716.4 58.5 %all-to-all-done.3 = f32[4,3,6,48,256]{4,3,2,1,0:T(8,128)} async-done(((f32[4,3,6,48,256]{4,3,2,1,0:T(8,128)}), f32[4,3,6,48,256]{4,3,2,1,0:T(8,128)}, u32[]{:S(2)}, u32[]{:S(2)}) %all-to-all-start.3) | async-done | bytes 3538976 | tf_op jit(solution)/shard_map/all_to_all | solution.py:265
  778.2 13.3 %multiply_add_fusion = f32[3,6,48,1024]{3,2,1,0:T(8,128)} fusion(f32[3,6,48,1024]{3,2,1,0:T(8,128)S(1)} %copy-done, f32[3,6,48,1024]{3,2,1,0:T(8,128)S(1)} %bitcast.226, f32[1024,1024,1,1]{1,0,3,2:T(8,128)S(1)} %copy-done.8), kind=kOutput, calls=%fused_computation.111 | convolution fusion | flops 10873405440 | bytes 14811136 | tf_op jit(solution)/shard_map/dot_general | solution.py:267
  (203 shorter events, 172.1 us)
Async XLA Ops:
  0.7 65.1 %copy-start.33 = (pred[1024]{0:T(1024)(128)(4,1)}, pred[1024]{0:T(1024)(128)(4,1)S(1)}, u32[]{:S(2)}) copy-start(pred[1024]{0:T(1024)(128)(4,1)S(1)} %fusion.197) | copy-start | bytes 3076
  0.7 4.5 copy-start
  55.8 122.6 %all-to-all-start.1 = ((f32[4,1,221184]{2,1,0:T(1,128)}), f32[4,1,221184]{2,1,0:T(1,128)}, u32[]{:S(2)}, u32[]{:S(2)}) async-start(f32[4,1,221184]{2,1,0:T(1,128)} %reshape.519), calls=%async_computation.1 | async-start | bytes 7077888 | tf_op jit(solution)/shard_map/all_to_all | solution.py:185
  62.8 139.6 %collective-permute-start = (f32[3,3,48,1024]{3,2,1,0:T(8,128)}, f32[3,3,48,1024]{3,2,1,0:T(8,128)}, u32[]{:S(2)}, u32[]{:S(2)}) collective-permute-start(f32[3,3,48,1024]{3,2,1,0:T(8,128)} %get-tuple-element.34), channel_id=1, source_target_pairs={{0,4},{4,8},{8,12},{12,16},{16,20},{20,24},{24,28},{28,0},{1,5},{5... | collective-permute-start | bytes 5308424 | tf_op jit(solution)/shard_map/ppermute | solution.py:25
  64.7 141.1 %collective-permute-start.1 = (f32[3,3,48,1024]{3,2,1,0:T(8,128)}, f32[3,3,48,1024]{3,2,1,0:T(8,128)}, u32[]{:S(2)}, u32[]{:S(2)}) collective-permute-start(f32[3,3,48,1024]{3,2,1,0:T(8,128)} %get-tuple-element.33), channel_id=1, source_target_pairs={{4,0},{8,4},{12,8},{16,12},{20,16},{24,20},{28,24},{0,28},{5,1},{9... | collective-permute-start | bytes 5308424 | tf_op jit(solution)/shard_map/ppermute | solution.py:27
  166.0 3.3 copy-start.11
  178.4 99.0 %all-to-all-start.2 = ((f32[4,1,221184]{2,1,0:T(1,128)}), f32[4,1,221184]{2,1,0:T(1,128)}, u32[]{:S(2)}, u32[]{:S(2)}) async-start(f32[4,1,221184]{2,1,0:T(1,128)} %reshape.517), calls=%async_computation.2 | async-start | bytes 7077888 | tf_op jit(solution)/shard_map/all_to_all | solution.py:196
  216.4 8.3 %copy-start.34 = (pred[1024]{0:T(1024)(128)(4,1)S(1)}, pred[1024]{0:T(1024)(128)(4,1)}, u32[]{:S(2)}) copy-start(pred[1024]{0:T(1024)(128)(4,1)} %copy-done.33) | copy-start | bytes 3076
  277.3 207.1 %all-to-all-start = ((f32[4,1,221184]{2,1,0:T(1,128)}), f32[4,1,221184]{2,1,0:T(1,128)}, u32[]{:S(2)}, u32[]{:S(2)}) async-start(f32[4,1,221184]{2,1,0:T(1,128)} %reshape.521), calls=%async_computation | async-start | bytes 7077888 | tf_op jit(solution)/shard_map/all_to_all | solution.py:177
  347.6 6.5 copy-start.4
  448.0 6.5 copy-start.5
  548.8 6.5 copy-start.6
  559.7 2.0 copy-start.9
  559.7 3.1 copy-start.10
  563.5 2.5 copy-start.1
  563.5 3.6 copy-start.25
  566.1 1.0 copy-start.12
  568.0 28.1 %collective-permute-start.2 = (f32[2,1,192,256]{3,2,1,0:T(8,128)}, f32[2,1,192,256]{3,2,1,0:T(8,128)}, u32[]{:S(2)}, u32[]{:S(2)}) collective-permute-start(f32[2,1,192,256]{3,2,1,0:T(8,128)} %get-tuple-element.39), channel_id=1, source_target_pairs={{4,0},{8,4},{12,8},{16,12},{20,16},{24,20},{28,24},{0,28},{5,1},{9... | collective-permute-start | bytes 1179656 | tf_op jit(solution)/shard_map/ppermute | solution.py:27
  569.3 31.0 %collective-permute-start.3 = (f32[2,1,192,256]{3,2,1,0:T(8,128)}, f32[2,1,192,256]{3,2,1,0:T(8,128)}, u32[]{:S(2)}, u32[]{:S(2)}) collective-permute-start(f32[2,1,192,256]{3,2,1,0:T(8,128)} %get-tuple-element.40), channel_id=1, source_target_pairs={{0,4},{4,8},{8,12},{12,16},{16,20},{20,24},{24,28},{28,0},{1,5},{5... | collective-permute-start | bytes 1179656 | tf_op jit(solution)/shard_map/ppermute | solution.py:25
  603.7 4.1 copy-start.13
  603.7 4.1 copy-start.14
  603.7 4.1 copy-start.16
  603.7 4.1 copy-start.26
  603.7 4.1 copy-start.28
  607.9 3.3 copy-start.36
  609.3 1.0 copy-start.19
  611.2 13.1 %collective-permute-start.4 = (f32[1,1,192,256]{3,2,1,0:T(8,128)}, f32[1,1,192,256]{3,2,1,0:T(8,128)}, u32[]{:S(2)}, u32[]{:S(2)}) collective-permute-start(f32[1,1,192,256]{3,2,1,0:T(8,128)} %get-tuple-element.47), channel_id=1, source_target_pairs={{4,0},{8,4},{12,8},{16,12},{20,16},{24,20},{28,24},{0,28},{5,1},{9... | collective-permute-start | bytes 589832 | tf_op jit(solution)/shard_map/ppermute | solution.py:27
  615.8 15.1 %copy-start.30 = (f32[128]{0:T(128)S(1)}, f32[128]{0:T(128)}, u32[]{:S(2)}) copy-start(f32[128]{0:T(128)} %get-tuple-element.8) | copy-start | bytes 1540
  618.8 9.0 %collective-permute-start.5 = (f32[1,1,192,256]{3,2,1,0:T(8,128)}, f32[1,1,192,256]{3,2,1,0:T(8,128)}, u32[]{:S(2)}, u32[]{:S(2)}) collective-permute-start(f32[1,1,192,256]{3,2,1,0:T(8,128)} %get-tuple-element.48), channel_id=1, source_target_pairs={{0,4},{4,8},{8,12},{12,16},{16,20},{20,24},{24,28},{28,0},{1,5},{5... | collective-permute-start | bytes 589832 | tf_op jit(solution)/shard_map/ppermute | solution.py:25
  629.5 4.7 copy-start.7
  629.5 4.7 copy-start.20
  629.5 4.7 copy-start.27
  629.5 4.7 copy-start.29
  634.2 3.8 copy-start.15
  634.2 3.8 copy-start.17
  642.2 8.6 %copy-start.37 = (f32[128]{0:T(128)S(1)}, f32[128]{0:T(128)}, u32[]{:S(2)}) copy-start(f32[128]{0:T(128)} %get-tuple-element.89) | copy-start | bytes 1540
  642.2 8.6 %copy-start.38 = (f32[128]{0:T(128)S(1)}, f32[128]{0:T(128)}, u32[]{:S(2)}) copy-start(f32[128]{0:T(128)} %fusion.285) | copy-start | bytes 1540
  644.0 21.0 %collective-permute-start.6 = (f32[1,1,192,256]{3,2,1,0:T(8,128)}, f32[1,1,192,256]{3,2,1,0:T(8,128)}, u32[]{:S(2)}, u32[]{:S(2)}) collective-permute-start(f32[1,1,192,256]{3,2,1,0:T(8,128)} %get-tuple-element.41), channel_id=1, source_target_pairs={{4,0},{8,4},{12,8},{16,12},{20,16},{24,20},{28,24},{0,28},{5,1},{9... | collective-permute-start | bytes 589832 | tf_op jit(solution)/shard_map/ppermute | solution.py:27
  644.0 24.6 %collective-permute-start.7 = (f32[1,1,192,256]{3,2,1,0:T(8,128)}, f32[1,1,192,256]{3,2,1,0:T(8,128)}, u32[]{:S(2)}, u32[]{:S(2)}) collective-permute-start(f32[1,1,192,256]{3,2,1,0:T(8,128)} %get-tuple-element.42), channel_id=1, source_target_pairs={{0,4},{4,8},{8,12},{12,16},{16,20},{20,24},{24,28},{28,0},{1,5},{5... | collective-permute-start | bytes 589832 | tf_op jit(solution)/shard_map/ppermute | solution.py:25
  658.5 13.2 %copy-start.31 = (f32[128]{0:T(128)S(1)}, f32[128]{0:T(128)}, u32[]{:S(2)}) copy-start(f32[128]{0:T(128)} %get-tuple-element.9) | copy-start | bytes 1540
  658.5 13.2 %copy-start.32 = (f32[128]{0:T(128)S(1)}, f32[128]{0:T(128)}, u32[]{:S(2)}) copy-start(f32[128]{0:T(128)} %get-tuple-element.87) | copy-start | bytes 1540
  670.3 6.9 copy-start.2
  670.3 6.9 copy-start.23
  670.3 6.9 copy-start.24
  680.1 4.4 copy-start.3
  691.7 5.2 copy-start.35
  691.7 83.2 %all-to-all-start.3 = ((f32[4,3,6,48,256]{4,3,2,1,0:T(8,128)}), f32[4,3,6,48,256]{4,3,2,1,0:T(8,128)}, u32[]{:S(2)}, u32[]{:S(2)}) async-start(f32[4,3,6,48,256]{4,3,2,1,0:T(8,128)} %pad_maximum_fusion.8), calls=%async_computation.3 | async-start | bytes 7077888 | tf_op jit(solution)/shard_map/all_to_all | solution.py:265
  774.9 3.3 copy-start.8
  (3 other events, 2.8 us)
